TPU v7x, 128 devices: a whole 4x4x4 slice. The times are simulated.
128 devices in a mesh: row: 8 (over z, core), col: 16 (over y, x).
Axes of the slice: x: 4, y: 4, z: 4, core: 2. Of those that a mesh axis runs over, the one named last changes fastest.
Arguments:
- grad_out: bfloat16 [131072, 256], P(('row', 'col')), may hold values from -6 to 6
- rel_weight: bfloat16 [4, 256, 256], replicated, may hold values from -0.375 to 0.375
- adjacency: bfloat16 [24576, 128, 128], P(('row', 'col')), may hold values from -0.5 to 0.5
- block_row: int32 [24576], P(('row', 'col')), may hold values from 0 to 127, as said below
- block_col: int32 [24576], P(('row', 'col')), may hold values from 0 to 63
- type_count: int32 [512], P(('row', 'col')), may hold values from 0 to 192, as said below
Outputs:
- grad_in: float32 [131072, 256], P(('row', 'col'))
Inputs may be any that keep to these rules, and one draw needn't show every extreme that they name: `block_row`: among all 192 slots of one tile, at most 4 distinct values fall in any aligned range of 8 values (the node blocks of one device of the tile row), and in every tile some range holds exactly 4. `type_count`: A tile's 4 counts sum to at most 192; in some tile a single type holds all 192 slots.
All inputs are finite; a program needn't handle non-finite values.
Results may differ from a plain program's by a relative error of at most 0.012.
Values may be sent and summed in bfloat16 or wider, within the bound.
A program may use at most 192 MiB of HBM per device.

v0:
```python
import math

import jax
import jax.numpy as jnp
from jax import lax
from jax.sharding import PartitionSpec as P


def per_device(grad_out, rel_weight, adjacency, block_row, block_col, type_count):
    ncols = lax.axis_size("col")
    nrows = lax.axis_size("row")
    blk = adjacency.shape[1]
    feat = grad_out.shape[1]
    kinds = rel_weight.shape[0]
    owned = grad_out.shape[0] // blk
    slots_total = adjacency.shape[0]
    wcat = jnp.transpose(rel_weight, (2, 0, 1)).reshape(feat, kinds * feat)
    gathered = jnp.dot(
        lax.all_gather(grad_out, "col", axis=0, tiled=True),
        wcat,
        preferred_element_type=jnp.float32,
    ).astype(jnp.bfloat16)
    table = gathered.reshape(ncols * owned, blk, kinds, feat)
    ends = jnp.cumsum(type_count)
    total = ends[kinds - 1]
    position = jnp.arange(slots_total, dtype=jnp.int32)
    kind = jnp.minimum(
        jnp.sum((position[:, None] >= ends[None, :]).astype(jnp.int32), axis=1), kinds - 1
    )
    live = position < total
    group = math.gcd(slots_total, 64)
    groups = slots_total // group
    partial_start = jnp.zeros((nrows * owned, blk, feat), jnp.float32)

    def step(index, partial_value):
        start = index * group
        adj_part = lax.dynamic_slice_in_dim(adjacency, start, group, 0)
        slot_part = lax.dynamic_slice_in_dim(block_row, start, group, 0)
        kind_part = lax.dynamic_slice_in_dim(kind, start, group, 0)
        live_part = lax.dynamic_slice_in_dim(live, start, group, 0)
        col_part = lax.dynamic_slice_in_dim(block_col, start, group, 0)
        picked = table[slot_part, :, kind_part, :]
        term = jnp.einsum("kab,kaf->kbf", adj_part, picked, preferred_element_type=jnp.float32)
        term = jnp.where(live_part[:, None, None], term, jnp.float32(0.0))
        return partial_value.at[col_part].add(term)

    partial_value = lax.fori_loop(0, groups, step, partial_start)
    return lax.psum_scatter(
        partial_value.reshape(nrows * owned * blk, feat).astype(jnp.bfloat16),
        "row",
        scatter_dimension=0,
        tiled=True,
    ).astype(jnp.float32)


def solution(mesh):
    in_specs = (
        P(("row", "col"), None),
        P(),
        P(("row", "col"), None, None),
        P(("row", "col")),
        P(("row", "col")),
        P(("row", "col")),
    )
    out_specs = P(("row", "col"), None)
    return jax.shard_map(
        per_device, mesh=mesh, in_specs=in_specs, out_specs=out_specs, check_vma=False
    )
```

profile of v0, /device:TPU:1, one launch (start us, length us, event | category | flops | bytes accessed | tf_op | source)
XLA Modules:
  0.0 330.3 jit_solution(6268306720380920505)
XLA Ops:
  6.5 0.0 copy-start
  6.5 0.0 all-gather.2.cloned.1.call-start
  6.5 0.7 all-gather.2.cloned.1.call-update
  7.3 0.0 reduce-scatter.2.cloned.1.call-start
  7.3 0.8 reduce-window.4
  8.1 0.6 slice.4
  8.7 0.6 iota_compare_fusion.1
  9.3 0.1 convert_reduce_fusion
  9.4 73.8 %all-gather.2.cloned.1.call-done = bf16[16384,256]{1,0:T(8,128)(2,1)} async-done(((bf16[1024,256]{1,0:T(8,128)(2,1)}), bf16[16384,256]{1,0:T(8,128)(2,1)}) %all-gather.2.cloned.1.call-update) | async-done | bytes 8388624 | tf_op jit(solution)/shard_map/all_gather | solution.py:19
  83.2 0.0 copy-done
  83.2 17.5 %convolution_convert_fusion = bf16[16384,1024]{1,0:T(8,128)(2,1)} fusion(bf16[16384,256]{1,0:T(8,128)(2,1)} %all-gather.2.cloned.1.call-done, bf16[256,1024]{0,1:T(8,128)(2,1)S(1)} %bitcast.12), kind=kOutput, calls=%fused_computation.13 | convolution fusion | flops 8606711808 | bytes 42467328 | tf_op jit(solution)/shard_map/dot_general | solution.py:18
  100.7 54.7 %reshape.19 = bf16[128,128,4,256]{3,2,1,0:T(4,128)(2,1)} reshape(bf16[16384,1024]{1,0:T(8,128)(2,1)} %convolution_convert_fusion) | data formatting | bytes 67108864 | tf_op jit(solution)/shard_map/reshape | solution.py:23
  155.3 23.0 %copy.12 = bf16[128,128,4,256]{3,1,2,0:T(8,128)(2,1)} copy(bf16[128,128,4,256]{3,2,1,0:T(4,128)(2,1)} %reshape.19) | data formatting | bytes 67108864 | tf_op jit(solution)/shard_map/while | solution.py:47
  178.4 0.0 copy-start.2
  178.4 0.0 copy-start.3
  178.4 4.2 %broadcast_in_dim.53 = f32[64,128,256]{2,1,0:T(8,128)} broadcast(f32[]{:T(128)} %constant.55.clone.1), dimensions={} | broadcast | bytes 8388612 | tf_op jit(solution)/shard_map/broadcast_in_dim | solution.py:33
  182.6 0.0 copy-done.2
  182.6 0.0 copy-done.3
  182.6 97.2 %while.13 = (s32[]{:T(128)}, f32[64,128,256]{2,1,0:T(8,128)}, s32[192]{0:T(256)S(1)}, pred[192]{0:T(512)(128)(4,1)S(1)}, bf16[192,128,128]{2,1,0:T(8,128)(2,1)},...) while((s32[]{:T(128)}, f32[64,128,256]{2,1,0:T(8,128)}, ...), condition=%wide.region_4.5_spmd, body=%wide.region_2.4_spmd.sunk | while | flops 541066112 | bytes 48236912 | solution.py:47
  182.6 0.1 compare_select_fusion.4
  182.7 5.1 %gather_fusion = bf16[64,128,256]{2,1,0:T(8,128)(2,1)} fusion(bf16[128,128,4,256]{3,1,2,0:T(8,128)(2,1)} %get-tuple-element.271, s32[64]{0:T(128)S(1)} %get-tuple-element.239), kind=kCustom, calls=%fused_computation.clone.1 | custom fusion | bytes 8389120 | tf_op jit(solution)/shard_map/while/body/eval_jaxpr/gather | solution.py:42
  187.8 0.1 dynamic_slice.45
  187.9 7.6 %broadcast_select_fusion.2 = f32[64,128,256]{2,1,0:T(8,128)} fusion(pred[64]{0:T(512)(128)(4,1)S(1)} %dynamic_slice.45, bf16[64,128,256]{2,1,0:T(8,128)(2,1)} %gather_fusion, bf16[192,128,128]{2,1,0:T(8,128)(2,1)} %get-tuple-element.268, s32[]{:T(128)S(6)} %select_n.61), kind=kOutput, calls=%fused_computation.2.clone.1 | convolution fusion | flops 538968064 | bytes 14680132 | tf_op jit(solution)/shard_map/while/body/eval_jaxpr/kab,kaf->kbf/dot_general | solution.py:43
  195.4 19.5 %scatter_fusion = f32[64,128,256]{2,1,0:T(8,128)} fusion(f32[64,128,256]{2,1,0:T(8,128)} %get-tuple-element.253, s32[64]{0:T(128)S(1)} %get-tuple-element.238, f32[64,128,256]{2,1,0:T(8,128)} %broadcast_select_fusion.2), kind=kCustom, calls=%fused_computation.1.clone.1 | custom fusion | flops 2097152 | bytes 25166080 | tf_op jit(solution)/shard_map/while/body/eval_jaxpr/scatter-add | solution.py:45
  214.9 0.1 compare_select_fusion.4
  215.0 5.2 %gather_fusion = bf16[64,128,256]{2,1,0:T(8,128)(2,1)} fusion(bf16[128,128,4,256]{3,1,2,0:T(8,128)(2,1)} %get-tuple-element.271, s32[64]{0:T(128)S(1)} %get-tuple-element.239), kind=kCustom, calls=%fused_computation.clone.1 | custom fusion | bytes 8389120 | tf_op jit(solution)/shard_map/while/body/eval_jaxpr/gather | solution.py:42
  220.2 0.1 dynamic_slice.45
  220.3 7.6 %broadcast_select_fusion.2 = f32[64,128,256]{2,1,0:T(8,128)} fusion(pred[64]{0:T(512)(128)(4,1)S(1)} %dynamic_slice.45, bf16[64,128,256]{2,1,0:T(8,128)(2,1)} %gather_fusion, bf16[192,128,128]{2,1,0:T(8,128)(2,1)} %get-tuple-element.268, s32[]{:T(128)S(6)} %select_n.61), kind=kOutput, calls=%fused_computation.2.clone.1 | convolution fusion | flops 538968064 | bytes 14680132 | tf_op jit(solution)/shard_map/while/body/eval_jaxpr/kab,kaf->kbf/dot_general | solution.py:43
  227.9 19.6 %scatter_fusion = f32[64,128,256]{2,1,0:T(8,128)} fusion(f32[64,128,256]{2,1,0:T(8,128)} %get-tuple-element.253, s32[64]{0:T(128)S(1)} %get-tuple-element.238, f32[64,128,256]{2,1,0:T(8,128)} %broadcast_select_fusion.2), kind=kCustom, calls=%fused_computation.1.clone.1 | custom fusion | flops 2097152 | bytes 25166080 | tf_op jit(solution)/shard_map/while/body/eval_jaxpr/scatter-add | solution.py:45
  247.4 0.1 compare_select_fusion.4
  247.5 5.4 %gather_fusion = bf16[64,128,256]{2,1,0:T(8,128)(2,1)} fusion(bf16[128,128,4,256]{3,1,2,0:T(8,128)(2,1)} %get-tuple-element.271, s32[64]{0:T(128)S(1)} %get-tuple-element.239), kind=kCustom, calls=%fused_computation.clone.1 | custom fusion | bytes 8389120 | tf_op jit(solution)/shard_map/while/body/eval_jaxpr/gather | solution.py:42
  252.9 0.1 dynamic_slice.45
  253.0 7.6 %broadcast_select_fusion.2 = f32[64,128,256]{2,1,0:T(8,128)} fusion(pred[64]{0:T(512)(128)(4,1)S(1)} %dynamic_slice.45, bf16[64,128,256]{2,1,0:T(8,128)(2,1)} %gather_fusion, bf16[192,128,128]{2,1,0:T(8,128)(2,1)} %get-tuple-element.268, s32[]{:T(128)S(6)} %select_n.61), kind=kOutput, calls=%fused_computation.2.clone.1 | convolution fusion | flops 538968064 | bytes 14680132 | tf_op jit(solution)/shard_map/while/body/eval_jaxpr/kab,kaf->kbf/dot_general | solution.py:43
  260.6 19.3 %scatter_fusion = f32[64,128,256]{2,1,0:T(8,128)} fusion(f32[64,128,256]{2,1,0:T(8,128)} %get-tuple-element.253, s32[64]{0:T(128)S(1)} %get-tuple-element.238, f32[64,128,256]{2,1,0:T(8,128)} %broadcast_select_fusion.2), kind=kCustom, calls=%fused_computation.1.clone.1 | custom fusion | flops 2097152 | bytes 25166080 | tf_op jit(solution)/shard_map/while/body/eval_jaxpr/scatter-add | solution.py:45
  279.9 0.0 copy-start.1
  279.9 6.0 %convert_element_type.17 = bf16[64,128,256]{2,1,0:T(8,128)(2,1)} convert(f32[64,128,256]{2,1,0:T(8,128)} %get-tuple-element.144) | non-fusion elementwise | flops 2097152 | bytes 12582912 | tf_op jit(solution)/shard_map/convert_element_type | solution.py:49
  285.9 0.0 reduce-scatter.2.cloned.1.call-update
  285.9 35.5 %reduce-scatter.2.cloned.1.call-done = bf16[1024,256]{1,0:T(8,128)(2,1)} async-done(((bf16[8192,256]{1,0:T(8,128)(2,1)}), bf16[1024,256]{1,0:T(8,128)(2,1)}) %reduce-scatter.2.cloned.1.call-update) | async-done | bytes 524304 | tf_op jit(solution)/shard_map/reduce_scatter | solution.py:48
  321.4 2.1 convert_element_type.19
  323.5 0.0 copy-done.1
  (1 shorter events, 0.0 us)
Async XLA Ops:
  6.5 76.7 %copy-start = (bf16[4,256,256]{2,1,0:T(8,128)(2,1)S(1)}, bf16[4,256,256]{2,1,0:T(8,128)(2,1)}, u32[]{:S(2)}) copy-start(bf16[4,256,256]{2,1,0:T(8,128)(2,1)} %param.9) | copy-start | bytes 1572868
  6.5 76.7 %all-gather.2.cloned.1.call-start = ((), (), s32[]{:S(2)}) async-start(), calls=%async_computation.1 | async-start | bytes 8912896 | tf_op jit(solution)/shard_map/all_gather | solution.py:19
  7.3 314.1 %reduce-scatter.2.cloned.1.call-start = ((), (), s32[]{:S(2)}) async-start(), calls=%async_computation.2 | async-start | bytes 4718592 | tf_op jit(solution)/shard_map/reduce_scatter | solution.py:48
  178.4 4.2 %copy-start.2 = (s32[192]{0:T(256)S(1)}, s32[192]{0:T(256)}, u32[]{:S(2)}) copy-start(s32[192]{0:T(256)} %param.12) | copy-start | bytes 2308
  178.4 4.2 %copy-start.3 = (s32[192]{0:T(256)S(1)}, s32[192]{0:T(256)}, u32[]{:S(2)}) copy-start(s32[192]{0:T(256)} %param.11) | copy-start | bytes 2308
  279.9 43.6 %copy-start.1 = (bf16[4,256,256]{2,1,0:T(8,128)(2,1)S(1)}, bf16[4,256,256]{2,1,0:T(8,128)(2,1)}, u32[]{:S(2)}) copy-start(bf16[4,256,256]{2,1,0:T(8,128)(2,1)} %param.9) | copy-start | bytes 1572868
Sparse Core Ops, SparseCore 0:
  9.5 73.6 all-gather.1
  286.0 35.3 reduce-scatter.1
where the time goes:
time: 334 us; the launch traced here: 330 us
  waiting for transfers between devices  110 us (33%)
  local copies, waits for them, and re-layouts  98.5 us (29%)
  other arithmetic  68.2 us (20%)
  matrix products  40.1 us (12%)
  between operations  13.4 us (4%)
    all_gather x1, waiting for transfers between devices, per_device(): lax.all_gather(grad_out, 'col', axis=0, tiled=True)  73.8 us
    scatter-add x3, other arithmetic, step(): return partial_value.at[col_part].add(term)  58.4 us
    reshape x1, local copies, waits for them, and re-layouts, per_device(): table = gathered.reshape(ncols * owned, blk, kinds, feat)  54.7 us
    reduce_scatter x1, waiting for transfers between devices, per_device(): lax.psum_scatter(partial_value.reshape(nrows * owned * blk, feat).astype(...  35.5 us
    while x1, local copies, waits for them, and re-layouts, per_device(): partial_value = lax.fori_loop(0, groups, step, partial_start)  23 us
    dot_general x3, matrix products, step(): jnp.einsum('kab,kaf->kbf', adj_part, picked, preferred_element_type=jnp.f...  22.7 us
    dot_general x1, matrix products, per_device(): jnp.dot(lax.all_gather(grad_out, 'col', axis=0, tiled=True), wcat, prefer...  17.5 us
    gather x3, local copies, waits for them, and re-layouts, step(): picked = table[slot_part, :, kind_part, :]  15.7 us
  transfers between devices with their start and end apart: 2, of which 2 were waited for; matrix products, arithmetic and copies ran while one was open for 1% of the time, Pallas kernels for 0%

commit v1 on v0

v1 whole, which is shorter than its diff:
```python
import jax
import jax.numpy as jnp
from jax import lax
from jax.experimental import pallas as pl
from jax.experimental.pallas import tpu as pltpu
from jax.sharding import PartitionSpec as P

MESH = pl.DeviceIdType.MESH
RING = 4
BLK = 128
HALF = 64
F = 256
OWN = 8
CAP = 4
TYPES = 4
SLOTS = 192
PAIRS = 128
COLS = 64
NCOPY = 62
NRS = 10


def kernel(order_s, tsel_s, keep_s, last_s, need_s, need_v, g_ref, w_ref, a_hbm, out_ref,
           g01, g02, g03, g11, g12, g13, p0, p1, rl0, rl1, pk0, pk1, needs_v, needs_s,
           wt, a_v, at, table, acc, prefix, ps, pr, ss, zr, zf,
           send_sem, recv_sem, rs_send, rs_recv, local_sem):
    row = lax.axis_index("row")
    col = lax.axis_index("col")
    y, x = col // RING, lax.rem(col, RING)
    z, core = row // 2, lax.rem(row, 2)
    full = ((None, g01, g02, g03), (None, g11, g12, g13))
    packed = (p0, p1)
    relay = (rl0, rl1)
    outbox = (pk0, pk1)

    def at_xy(dx, dy):
        return lax.rem(y + dy, RING) * RING + lax.rem(x + dx, RING)

    def at_uv(h, du, dv):
        return at_xy(du, dv) if h == 0 else at_xy(dv, du)

    def dev_uv(h, du, dv):
        return (row, at_uv(h, du, dv))

    def dev_z(dz):
        return (lax.rem(z + dz, RING) * 2 + core, col)

    partner = (z * 2 + (1 - core), col)

    counter = [0]
    copies = {}

    def send(name, src, dst, dev):
        k = counter[0]
        counter[0] += 1
        c = pltpu.make_async_remote_copy(
            src_ref=src, dst_ref=dst, send_sem=send_sem.at[k], recv_sem=recv_sem.at[k],
            device_id=dev, device_id_type=MESH)
        c.start()
        copies[name] = c

    def got(name):
        copies[name].wait_recv()

    a_copy = pltpu.make_async_copy(a_hbm, a_v.at[pl.ds(0, SLOTS)], local_sem.at[0])
    a_copy.start()

    barrier = pltpu.get_barrier_semaphore()
    greeted = [dev_uv(h, 0, d) for h in (0, 1) for d in (1, 2, 3)] + [dev_z(1), dev_z(3), partner]
    for dev in greeted:
        pl.semaphore_signal(barrier, inc=1, device_id=dev, device_id_type=MESH)
    pl.semaphore_wait(barrier, len(greeted))

    for h in (0, 1):
        for d in (1, 2, 3):
            send(("need", h, d), need_v, needs_v.at[h * 3 + (4 - d) - 1], dev_uv(h, 0, d))
    for s in (1, 3):
        for h in (0, 1):
            send(("p1", h, s), g_ref.at[:, h], full[h][4 - s], dev_uv(h, s, 0))

    for t in range(TYPES):
        wt[:, t * F:(t + 1) * F] = w_ref[t].T
    a_v[SLOTS] = jnp.zeros((BLK, BLK), jnp.bfloat16)
    prefix[PAIRS] = jnp.zeros((BLK, F), jnp.bfloat16)

    for h in (0, 1):
        for d in (1, 2, 3):
            got(("need", h, d))
    need_copy = pltpu.make_async_copy(needs_v, needs_s, local_sem.at[1])
    need_copy.start()
    need_copy.wait()

    def pick(h, du, b):
        return g_ref[b, h] if du == 0 else full[h][du][b]

    def push(h, du):
        src = at_uv(h, du, 0)
        for dv in (2, 1, 3):
            for pos in range(CAP):
                b = needs_s[h * 3 + dv - 1, 0, src * CAP + pos]
                outbox[h][du, dv - 1, pos] = pick(h, du, b)
            if dv == 2:
                send(("rl", h, 0, du), outbox[h].at[du, 1, pl.ds(0, 2)], relay[h].at[0, du], dev_uv(h, 0, 1))
                send(("rl", h, 1, du), outbox[h].at[du, 1, pl.ds(2, 2)], relay[h].at[1, du], dev_uv(h, 0, 3))
            else:
                send(("p2", h, dv, du), outbox[h].at[du, dv - 1], packed[h].at[4 - dv - 1, du], dev_uv(h, 0, dv))

    def forward(h, du):
        got(("rl", h, 0, du))
        send(("fw", h, 0, du), relay[h].at[0, du], packed[h].at[1, du, pl.ds(0, 2)], dev_uv(h, 0, 1))
        got(("rl", h, 1, du))
        send(("fw", h, 1, du), relay[h].at[1, du], packed[h].at[1, du, pl.ds(2, 2)], dev_uv(h, 0, 3))

    def arrive(h, du, dv):
        if dv == 0:
            return
        if dv == 2:
            got(("fw", h, 0, du))
            got(("fw", h, 1, du))
        else:
            got(("p2", h, 4 - dv, du))

    def make_table(dy, dx):
        arrive(0, dx, dy)
        arrive(1, dy, dx)
        src = at_xy(dx, dy)
        rel = dy * RING + dx

        def piece(h, du, dv, pos):
            if dv == 0:
                return pick(h, du, need_s[src * CAP + pos])
            return packed[h][dv - 1, du, pos]

        def body(pos, carry):
            blk = jnp.concatenate([piece(0, dx, dy, pos), piece(1, dy, dx, pos)], axis=0)
            for t in range(TYPES):
                table[rel * CAP * TYPES + pos * TYPES + t] = jnp.dot(
                    blk, wt[:, t * F:(t + 1) * F], preferred_element_type=jnp.float32).astype(jnp.bfloat16)
            return carry

        lax.fori_loop(0, CAP, body, 0)

    def turn(start, stop):
        def body(p, carry):
            at[p, :, 0:BLK] = a_v[order_s[2 * p]].T
            at[p, :, BLK:2 * BLK] = a_v[order_s[2 * p + 1]].T
            return carry

        lax.fori_loop(start, stop, body, 0)

    push(0, 0)
    push(1, 0)
    make_table(0, 0)
    a_copy.wait()
    for s in (1, 3):
        for h in (0, 1):
            got(("p1", h, s))
            lo = 0 if s == 1 else 4
            send(("p1r", h, s), full[h][4 - s].at[pl.ds(lo, 4)], full[h][2].at[pl.ds(lo, 4)], dev_uv(h, s, 0))
    for du in (3, 1):
        push(0, du)
        push(1, du)
    forward(0, 0)
    forward(1, 0)
    turn(0, 48)
    for h in (0, 1):
        for s in (1, 3):
            got(("p1r", h, s))
    push(0, 2)
    push(1, 2)
    for dy, dx in ((0, 1), (0, 3), (1, 0), (3, 0)):
        make_table(dy, dx)
    for du in (3, 1):
        forward(0, du)
        forward(1, du)
    turn(48, 96)
    for dy, dx in ((1, 1), (1, 3), (3, 1), (3, 3)):
        make_table(dy, dx)
    forward(0, 2)
    forward(1, 2)
    turn(96, PAIRS)
    for dy, dx in ((0, 2), (2, 0), (1, 2), (3, 2), (2, 1), (2, 3), (2, 2)):
        make_table(dy, dx)

    acc[...] = jnp.zeros_like(acc)

    def step(p, carry):
        rhs = jnp.concatenate([table[tsel_s[2 * p]], table[tsel_s[2 * p + 1]]], axis=0)
        d = jnp.dot(at[p], rhs, preferred_element_type=jnp.float32)
        keep = jnp.full((BLK, F), keep_s[p], jnp.int32) != 0
        total = jnp.where(keep, acc[...], 0.0) + d
        acc[...] = total
        prefix[p] = total.astype(jnp.bfloat16)
        return carry

    lax.fori_loop(0, PAIRS, step, 0)

    def mine(dz, c, b):
        return prefix[last_s[(lax.rem(z + dz, RING) * 2 + c) * OWN + b]]

    rs_counter = [0]
    rs = {}

    def rsend(name, src, dst, dev):
        k = rs_counter[0]
        rs_counter[0] += 1
        c = pltpu.make_async_remote_copy(
            src_ref=src, dst_ref=dst, send_sem=rs_send.at[k], recv_sem=rs_recv.at[k],
            device_id=dev, device_id_type=MESH)
        c.start()
        rs[name] = c

    f32 = jnp.float32
    for dz in (2, 1, 3, 0):
        for b in range(OWN):
            ps[dz, b] = mine(dz, 1 - core, b)
        rsend(("pair", dz), ps.at[dz], pr.at[dz], partner)

    rs[("pair", 2)].wait_recv()
    for b in range(OWN):
        ss[1, b] = (mine(2, core, b).astype(f32) + pr[2, b].astype(f32)).astype(jnp.bfloat16)
    rsend("far0", ss.at[1, pl.ds(0, 4)], zr.at[0], dev_z(1))
    rsend("far1", ss.at[1, pl.ds(4, 4)], zr.at[1], dev_z(3))
    rs[("pair", 1)].wait_recv()
    for b in range(4, 8):
        ss[0, b] = (mine(1, core, b).astype(f32) + pr[1, b].astype(f32)).astype(jnp.bfloat16)
    rsend("up_b", ss.at[0, pl.ds(4, 4)], zf.at[0, pl.ds(4, 4)], dev_z(1))
    rs[("pair", 3)].wait_recv()
    for b in range(0, 4):
        ss[2, b] = (mine(3, core, b).astype(f32) + pr[3, b].astype(f32)).astype(jnp.bfloat16)
    rsend("down_a", ss.at[2, pl.ds(0, 4)], zf.at[1, pl.ds(0, 4)], dev_z(3))
    rs["far0"].wait_recv()
    for b in range(0, 4):
        ss[0, b] = (mine(1, core, b).astype(f32) + pr[1, b].astype(f32) + zr[0, b].astype(f32)).astype(jnp.bfloat16)
    rsend("up_a", ss.at[0, pl.ds(0, 4)], zf.at[0, pl.ds(0, 4)], dev_z(1))
    rs["far1"].wait_recv()
    for b in range(4, 8):
        ss[2, b] = (mine(3, core, b).astype(f32) + pr[3, b].astype(f32) + zr[1, b - 4].astype(f32)).astype(jnp.bfloat16)
    rsend("down_b", ss.at[2, pl.ds(4, 4)], zf.at[1, pl.ds(4, 4)], dev_z(3))
    rs[("pair", 0)].wait_recv()
    for b in range(OWN):
        out_ref[b] = mine(0, core, b).astype(f32) + pr[0, b].astype(f32)
    rs["up_b"].wait_recv()
    for b in range(4, 8):
        out_ref[b] = out_ref[b] + zf[0, b].astype(f32)
    rs["down_a"].wait_recv()
    for b in range(0, 4):
        out_ref[b] = out_ref[b] + zf[1, b].astype(f32)
    rs["up_a"].wait_recv()
    for b in range(0, 4):
        out_ref[b] = out_ref[b] + zf[0, b].astype(f32)
    rs["down_b"].wait_recv()
    for b in range(4, 8):
        out_ref[b] = out_ref[b] + zf[1, b].astype(f32)
    for c in copies.values():
        c.wait_send()
    for c in rs.values():
        c.wait_send()


def plan(block_row, block_col, type_count):
    i32 = jnp.int32
    col = lax.axis_index("col")
    y, x = col // RING, lax.rem(col, RING)
    k = jnp.arange(SLOTS, dtype=i32)
    e0 = type_count[0]
    e1 = e0 + type_count[1]
    e2 = e1 + type_count[2]
    e3 = e2 + type_count[3]
    kind = (k >= e0).astype(i32) + (k >= e1).astype(i32) + (k >= e2).astype(i32)
    live = k < e3
    r = jnp.arange(128, dtype=i32)
    present = jnp.any(block_row[None, :] == r[:, None], axis=1)
    same = (r[:, None] // OWN == r[None, :] // OWN) & (r[None, :] < r[:, None])
    place = jnp.sum((same & present[None, :]).astype(i32), axis=1)
    slot = jnp.arange(64, dtype=i32)
    hit = (r[None, :] // OWN == slot[:, None] // CAP) & (place[None, :] == slot[:, None] % CAP) & present[None, :]
    need = jnp.sum(jnp.where(hit, r[None, :] % OWN, 0), axis=1)
    rel = ((r // 32 - y) % RING) * RING + (r // OWN - x) % RING
    where_row = rel * CAP + place
    tk = jnp.sum(jnp.where(block_row[:, None] == r[None, :], where_row[None, :], 0), axis=1) * TYPES + kind
    c = jnp.arange(COLS, dtype=i32)
    count = jnp.sum(((block_col[None, :] == c[:, None]) & live[None, :]).astype(i32), axis=1)
    pairs = (count + 1) // 2
    start = jnp.sum(jnp.where(c[None, :] < c[:, None], pairs[None, :], 0), axis=1)
    rank = jnp.sum(((block_col[None, :] == block_col[:, None]) & live[None, :] & (k[None, :] < k[:, None])).astype(i32), axis=1)
    base = jnp.sum(jnp.where(c[None, :] < block_col[:, None], pairs[None, :], 0), axis=1)
    spot = jnp.where(live, 2 * base + rank, -1)
    oh = spot[None, :] == jnp.arange(2 * PAIRS, dtype=i32)[:, None]
    order = SLOTS - jnp.sum(jnp.where(oh, SLOTS - k[None, :], 0), axis=1)
    tsel = jnp.sum(jnp.where(oh, tk[None, :], 0), axis=1)
    p = jnp.arange(PAIRS, dtype=i32)
    first = jnp.any((start[None, :] == p[:, None]) & (pairs[None, :] > 0), axis=1)
    keep = 1 - first.astype(i32)
    last = jnp.where(pairs > 0, start + pairs - 1, PAIRS)
    return order, tsel, keep, last, need


def per_device(grad_out, rel_weight, adjacency, block_row, block_col, type_count):
    order, tsel, keep, last, need = plan(block_row, block_col, type_count)
    need_v = jnp.pad(need[None, :], ((0, 7), (0, 64)))
    bf = jnp.bfloat16
    smem = pl.BlockSpec(memory_space=pltpu.SMEM)
    vmem = pl.BlockSpec(memory_space=pltpu.VMEM)
    half = pltpu.VMEM((OWN, HALF, F), bf)
    out = pl.pallas_call(
        kernel,
        out_shape=jax.ShapeDtypeStruct((OWN, BLK, F), jnp.float32),
        in_specs=[smem] * 5 + [vmem] * 3 + [pl.BlockSpec(memory_space=pl.ANY)],
        out_specs=vmem,
        scratch_shapes=[half] * 6 + [
            pltpu.VMEM((3, RING, CAP, HALF, F), bf),
            pltpu.VMEM((3, RING, CAP, HALF, F), bf),
            pltpu.VMEM((2, RING, 2, HALF, F), bf),
            pltpu.VMEM((2, RING, 2, HALF, F), bf),
            pltpu.VMEM((RING, 3, CAP, HALF, F), bf),
            pltpu.VMEM((RING, 3, CAP, HALF, F), bf),
            pltpu.VMEM((6, 8, 128), jnp.int32),
            pltpu.SMEM((6, 8, 128), jnp.int32),
            pltpu.VMEM((F, TYPES * F), bf),
            pltpu.VMEM((SLOTS + 1, BLK, BLK), bf),
            pltpu.VMEM((PAIRS, BLK, 2 * BLK), bf),
            pltpu.VMEM((16 * CAP * TYPES, BLK, F), bf),
            pltpu.VMEM((BLK, F), jnp.float32),
            pltpu.VMEM((PAIRS + 1, BLK, F), bf),
            pltpu.VMEM((RING, OWN, BLK, F), bf),
            pltpu.VMEM((RING, OWN, BLK, F), bf),
            pltpu.VMEM((3, OWN, BLK, F), bf),
            pltpu.VMEM((2, 4, BLK, F), bf),
            pltpu.VMEM((2, OWN, BLK, F), bf),
            pltpu.SemaphoreType.DMA((NCOPY,)),
            pltpu.SemaphoreType.DMA((NCOPY,)),
            pltpu.SemaphoreType.DMA((NRS,)),
            pltpu.SemaphoreType.DMA((NRS,)),
            pltpu.SemaphoreType.DMA((2,)),
        ],
        compiler_params=pltpu.CompilerParams(
            collective_id=0, has_side_effects=True, vmem_limit_bytes=67043328),
    )(order, tsel, keep, last, need, need_v,
      grad_out.reshape(OWN, 2, HALF, F), rel_weight, adjacency)
    return out.reshape(OWN * BLK, F)


def solution(mesh):
    in_specs = (
        P(("row", "col"), None),
        P(),
        P(("row", "col"), None, None),
        P(("row", "col")),
        P(("row", "col")),
        P(("row", "col")),
    )
    out_specs = P(("row", "col"), None)
    return jax.shard_map(
        per_device, mesh=mesh, in_specs=in_specs, out_specs=out_specs, check_vma=False
    )
```

time: 334 us -> 106 us (0.32); the launches traced: 330 us -> 106 us
  waiting for transfers between devices: 110 us -> 0 us
  local copies, waits for them, and re-layouts: 98.5 us -> 4.33 us
  Pallas kernels: 0 us -> 91.1 us
  other arithmetic: 68.2 us -> 7.76 us
  matrix products: 40.1 us -> 0 us
  between operations: 13.4 us -> 2.62 us
    pallas_call x0 -> x1, Pallas kernels: none -> 91.1 us  [per_device(): pl.pallas_call(kernel, out_shape=jax.ShapeDtypeStruct((OWN, BLK, F), jnp....]
    all_gather x1 -> x0, waiting for transfers between devices: 73.8 us -> none  [per_device(): lax.all_gather(grad_out, 'col', axis=0, tiled=True)]
    scatter-add x3 -> x0, other arithmetic: 58.4 us -> none  [step(): return partial_value.at[col_part].add(term)]
    reshape x1 -> x0, local copies, waits for them, and re-layouts: 54.7 us -> none  [per_device(): table = gathered.reshape(ncols * owned, blk, kinds, feat)]
    dot_general x4 -> x0, matrix products: 40.1 us -> none  [the longest x3 22.7 us: step(): jnp.einsum('kab,kaf->kbf', adj_part, picked, preferred_element_type=jnp.f...]
    reduce_scatter x1 -> x0, waiting for transfers between devices: 35.5 us -> none  [per_device(): lax.psum_scatter(partial_value.reshape(nrows * owned * blk, feat).astype(...]
    while x1 -> x0, local copies, waits for them, and re-layouts: 23 us -> none  [per_device(): partial_value = lax.fori_loop(0, groups, step, partial_start)]
    gather x3 -> x0, local copies, waits for them, and re-layouts: 15.7 us -> none  [step(): picked = table[slot_part, :, kind_part, :]]
  transfers between devices with their start and end apart: 2 -> 0, of which waited for: 2 -> 0; matrix products, arithmetic and copies ran while one was open for 1% -> 0% of each run, Pallas kernels for 0% -> 0%
where the time goes in v1:
time: 106 us
  Pallas kernels  91.1 us (86%)
  other arithmetic  7.76 us (7%)
  local copies, waits for them, and re-layouts  4.33 us (4%)
  between operations  2.62 us (2%)
    pallas_call x1, Pallas kernels, per_device(): pl.pallas_call(kernel, out_shape=jax.ShapeDtypeStruct((OWN, BLK, F), jnp....  91.1 us
    unnamed x3, local copies, waits for them, and re-layouts  2.27 us

profile of v1, /device:TPU:1, one launch (start us, length us, event | category | flops | bytes accessed | tf_op | source)
XLA Modules:
  0.0 105.8 jit_solution(15818696638244221426)
XLA Ops:
  0.0 0.8 fusion.1
  0.8 0.2 convert_reduce_fusion.1
  1.0 0.9 select_reduce_fusion.2
  1.9 0.2 select_reduce_fusion.4.need_s
  2.1 0.0 copy-start
  2.1 1.5 %fusion.17 = (s32[1]{0:T(128)}, s32[1]{0:T(128)}, s32[1]{0:T(128)}, s32[1]{0:T(128)}) fusion(s32[4]{0:T(128)} %param.11), kind=kLoop, calls=%fused_computation.68 | loop fusion | bytes 32 | tf_op jit(solution)/shard_map/slice | solution.py:269
  6.1 0.6 fusion.9
  6.7 0.8 convert_reduce_fusion.2
  7.5 0.9 convert_reduce_fusion
  8.4 0.1 select_reduce_fusion.5
  8.5 0.1 fusion.6
  8.6 0.5 add_select_fusion.1.last_s
  9.1 0.6 convert_subtract_fusion.keep_s
  9.7 0.8 select_reduce_fusion.3
  10.5 0.7 select_reduce_fusion
  11.2 0.6 broadcast_subtract_fusion.order_s
  11.8 0.0 copy-done
  11.8 0.6 pad.4.need_v
  12.4 91.1 %shard_map.64 = f32[8,128,256]{2,1,0:T(8,128)} custom-call(s32[256]{0:T(256)} %broadcast_subtract_fusion.order_s, s32[256]{0:T(256)} %get-tuple-element.5.tsel_s, s32[128]{0:T(128)} %convert_subtract_fusion.keep_s, s32[64]{0:T(128)} %add_select_fusion.1.last_s, s32[64]{0:T(128)} %copy-done, s32[8,128]{1,0:T(8,128)} %pad.4.need_v, ...), custom_call_target="tpu_custom_call" | custom-call | tf_op jit(solution)/shard_map/pallas_call | solution.py:306
  103.6 2.3 %copy.8 = f32[1024,256]{1,0:T(8,128)} copy(f32[1024,256]{1,0:T(8,128)} %bitcast.7) | data formatting | bytes 2097152
  (7 shorter events, 0.1 us)
Async XLA Ops:
  2.1 9.8 %copy-start = (s32[64]{0:T(128)}, s32[64]{0:T(128)S(1)}, u32[]{:S(2)}) copy-start(s32[64]{0:T(128)S(1)} %select_reduce_fusion.4.need_s) | copy-start | bytes 772

commit v2 on v1

--- a/solution.py
+++ b/solution.py
@@ -20,7 +20,67 @@
 NRS = 10
 
 
-def kernel(order_s, tsel_s, keep_s, last_s, need_s, need_v, g_ref, w_ref, a_hbm, out_ref,
+def across(row_vec, depth):
+    return jnp.broadcast_to(row_vec, (depth, row_vec.shape[1])).T
+
+
+def lane_ids(shape):
+    return lax.broadcasted_iota(jnp.int32, shape, 1)
+
+
+def sub_ids(shape):
+    return lax.broadcasted_iota(jnp.int32, shape, 0)
+
+
+def total_of(mask, value):
+    return jnp.sum(jnp.where(mask, value, 0), axis=0, keepdims=True)
+
+
+def plan_needs(rows_row):
+    n = 128
+    rows_down = across(rows_row, 2 * n)[:, 0:n]
+    present = jnp.max(jnp.where(rows_down == lane_ids((2 * n, n)), 1, 0), axis=0, keepdims=True)
+    sub, lane = sub_ids((n, n)), lane_ids((n, n))
+    present_down = across(present, n)
+    place = total_of((sub // OWN == lane // OWN) & (sub < lane), present_down)
+    place_down = across(place, n)
+    hit = (sub // OWN == lane // CAP) & (place_down == lane % CAP) & (present_down > 0)
+    return place, total_of(hit, sub % OWN)
+
+
+def plan_slots(rows_row, cols_row, counts, place, y, x):
+    n, m = 128, 256
+    k = lane_ids((1, m))
+    e0 = counts[0]
+    e1 = e0 + counts[1]
+    e2 = e1 + counts[2]
+    e3 = e2 + counts[3]
+    one = lambda mask: jnp.where(mask, 1, 0)
+    kind = one(k >= e0) + one(k >= e1) + one(k >= e2)
+    live = k < e3
+    sub, lane = sub_ids((n, m)), lane_ids((n, m))
+    rel = lax.rem(sub // 32 + RING - y, RING) * RING + lax.rem(sub // OWN + 2 * RING - x, RING)
+    tk = total_of(rows_row == sub, rel * CAP + across(place, m)) * TYPES + kind
+    cols_down = across(cols_row, m)
+    ksub, klane = sub_ids((m, m)), lane_ids((m, m))
+    live_down = ksub < e3
+    count = total_of((cols_down[:, 0:n] == lane_ids((m, n))) & live_down[:, 0:n], 1)
+    pairs = (count + 1) // 2
+    pairs_down = across(pairs, m)
+    start = total_of(sub[:, 0:n] < lane[:, 0:n], pairs_down[:, 0:n])
+    base = total_of(sub < cols_row, pairs_down)
+    rank = total_of((cols_down == cols_row) & live_down & (ksub < klane), 1)
+    spot = jnp.where(live, 2 * base + rank, -1)
+    match = across(spot, m) == klane
+    order = SLOTS - total_of(match, SLOTS - ksub)
+    tsel = total_of(match, across(tk, m))
+    first = total_of((across(start, n) == lane[:, 0:n]) & (pairs_down[:, 0:n] > 0), 1)
+    last = jnp.where(pairs > 0, start + pairs - 1, PAIRS)
+    return order, tsel, 1 - first, last
+
+
+def kernel(counts_s, rows_ref, cols_ref, g_ref, w_ref, a_hbm, out_ref,
+           rc_v, idx_v, idx_s, need_v,
            g01, g02, g03, g11, g12, g13, p0, p1, rl0, rl1, pk0, pk1, needs_v, needs_s,
            wt, a_v, at, table, acc, prefix, ps, pr, ss, zr, zf,
            send_sem, recv_sem, rs_send, rs_recv, local_sem):
@@ -65,6 +125,15 @@
     a_copy = pltpu.make_async_copy(a_hbm, a_v.at[pl.ds(0, SLOTS)], local_sem.at[0])
     a_copy.start()
 
+    rc_v[...] = jnp.full((8, 256), -1, jnp.int32)
+    idx_v[...] = jnp.zeros((8, 256), jnp.int32)
+    need_v[...] = jnp.zeros((8, 128), jnp.int32)
+    rc_v[0:1, 0:SLOTS] = rows_ref[...]
+    rc_v[1:2, 0:SLOTS] = cols_ref[...]
+    rows_row, cols_row = rc_v[0:1, :], rc_v[1:2, :]
+    place, need = plan_needs(rows_row)
+    need_v[0:1, :] = need
+
     barrier = pltpu.get_barrier_semaphore()
     greeted = [dev_uv(h, 0, d) for h in (0, 1) for d in (1, 2, 3)] + [dev_z(1), dev_z(3), partner]
     for dev in greeted:
@@ -78,6 +147,14 @@
         for h in (0, 1):
             send(("p1", h, s), g_ref.at[:, h], full[h][4 - s], dev_uv(h, s, 0))
 
+    order, tsel, keep, last = plan_slots(rows_row, cols_row, counts_s, place, y, x)
+    idx_v[0:1, :] = order
+    idx_v[1:2, :] = tsel
+    idx_v[2:3, 0:128] = keep
+    idx_v[3:4, 0:128] = last
+    idx_v[4:5, 0:128] = need
+    idx_copy = pltpu.make_async_copy(idx_v, idx_s, local_sem.at[2])
+    idx_copy.start()
     for t in range(TYPES):
         wt[:, t * F:(t + 1) * F] = w_ref[t].T
     a_v[SLOTS] = jnp.zeros((BLK, BLK), jnp.bfloat16)
@@ -89,6 +166,7 @@
     need_copy = pltpu.make_async_copy(needs_v, needs_s, local_sem.at[1])
     need_copy.start()
     need_copy.wait()
+    idx_copy.wait()
 
     def pick(h, du, b):
         return g_ref[b, h] if du == 0 else full[h][du][b]
@@ -128,7 +206,7 @@
 
         def piece(h, du, dv, pos):
             if dv == 0:
-                return pick(h, du, need_s[src * CAP + pos])
+                return pick(h, du, idx_s[4, src * CAP + pos])
             return packed[h][dv - 1, du, pos]
 
         def body(pos, carry):
@@ -142,8 +220,8 @@
 
     def turn(start, stop):
         def body(p, carry):
-            at[p, :, 0:BLK] = a_v[order_s[2 * p]].T
-            at[p, :, BLK:2 * BLK] = a_v[order_s[2 * p + 1]].T
+            at[p, :, 0:BLK] = a_v[idx_s[0, 2 * p]].T
+            at[p, :, BLK:2 * BLK] = a_v[idx_s[0, 2 * p + 1]].T
             return carry
 
         lax.fori_loop(start, stop, body, 0)
@@ -185,18 +263,18 @@
     acc[...] = jnp.zeros_like(acc)
 
     def step(p, carry):
-        rhs = jnp.concatenate([table[tsel_s[2 * p]], table[tsel_s[2 * p + 1]]], axis=0)
+        rhs = jnp.concatenate([table[idx_s[1, 2 * p]], table[idx_s[1, 2 * p + 1]]], axis=0)
         d = jnp.dot(at[p], rhs, preferred_element_type=jnp.float32)
-        keep = jnp.full((BLK, F), keep_s[p], jnp.int32) != 0
+        keep = jnp.full((BLK, F), idx_s[2, p], jnp.int32) != 0
         total = jnp.where(keep, acc[...], 0.0) + d
         acc[...] = total
         prefix[p] = total.astype(jnp.bfloat16)
         return carry
 
-    lax.fori_loop(0, PAIRS, step, 0)
+    lax.fori_loop(0, PAIRS, step, 0, unroll=8)
 
     def mine(dz, c, b):
-        return prefix[last_s[(lax.rem(z + dz, RING) * 2 + c) * OWN + b]]
+        return prefix[idx_s[3, (lax.rem(z + dz, RING) * 2 + c) * OWN + b]]
 
     rs_counter = [0]
     rs = {}
@@ -258,47 +336,7 @@
         c.wait_send()
 
 
-def plan(block_row, block_col, type_count):
-    i32 = jnp.int32
-    col = lax.axis_index("col")
-    y, x = col // RING, lax.rem(col, RING)
-    k = jnp.arange(SLOTS, dtype=i32)
-    e0 = type_count[0]
-    e1 = e0 + type_count[1]
-    e2 = e1 + type_count[2]
-    e3 = e2 + type_count[3]
-    kind = (k >= e0).astype(i32) + (k >= e1).astype(i32) + (k >= e2).astype(i32)
-    live = k < e3
-    r = jnp.arange(128, dtype=i32)
-    present = jnp.any(block_row[None, :] == r[:, None], axis=1)
-    same = (r[:, None] // OWN == r[None, :] // OWN) & (r[None, :] < r[:, None])
-    place = jnp.sum((same & present[None, :]).astype(i32), axis=1)
-    slot = jnp.arange(64, dtype=i32)
-    hit = (r[None, :] // OWN == slot[:, None] // CAP) & (place[None, :] == slot[:, None] % CAP) & present[None, :]
-    need = jnp.sum(jnp.where(hit, r[None, :] % OWN, 0), axis=1)
-    rel = ((r // 32 - y) % RING) * RING + (r // OWN - x) % RING
-    where_row = rel * CAP + place
-    tk = jnp.sum(jnp.where(block_row[:, None] == r[None, :], where_row[None, :], 0), axis=1) * TYPES + kind
-    c = jnp.arange(COLS, dtype=i32)
-    count = jnp.sum(((block_col[None, :] == c[:, None]) & live[None, :]).astype(i32), axis=1)
-    pairs = (count + 1) // 2
-    start = jnp.sum(jnp.where(c[None, :] < c[:, None], pairs[None, :], 0), axis=1)
-    rank = jnp.sum(((block_col[None, :] == block_col[:, None]) & live[None, :] & (k[None, :] < k[:, None])).astype(i32), axis=1)
-    base = jnp.sum(jnp.where(c[None, :] < block_col[:, None], pairs[None, :], 0), axis=1)
-    spot = jnp.where(live, 2 * base + rank, -1)
-    oh = spot[None, :] == jnp.arange(2 * PAIRS, dtype=i32)[:, None]
-    order = SLOTS - jnp.sum(jnp.where(oh, SLOTS - k[None, :], 0), axis=1)
-    tsel = jnp.sum(jnp.where(oh, tk[None, :], 0), axis=1)
-    p = jnp.arange(PAIRS, dtype=i32)
-    first = jnp.any((start[None, :] == p[:, None]) & (pairs[None, :] > 0), axis=1)
-    keep = 1 - first.astype(i32)
-    last = jnp.where(pairs > 0, start + pairs - 1, PAIRS)
-    return order, tsel, keep, last, need
-
-
 def per_device(grad_out, rel_weight, adjacency, block_row, block_col, type_count):
-    order, tsel, keep, last, need = plan(block_row, block_col, type_count)
-    need_v = jnp.pad(need[None, :], ((0, 7), (0, 64)))
     bf = jnp.bfloat16
     smem = pl.BlockSpec(memory_space=pltpu.SMEM)
     vmem = pl.BlockSpec(memory_space=pltpu.VMEM)
@@ -306,9 +344,14 @@
     out = pl.pallas_call(
         kernel,
         out_shape=jax.ShapeDtypeStruct((OWN, BLK, F), jnp.float32),
-        in_specs=[smem] * 5 + [vmem] * 3 + [pl.BlockSpec(memory_space=pl.ANY)],
+        in_specs=[smem] + [vmem] * 4 + [pl.BlockSpec(memory_space=pl.ANY)],
         out_specs=vmem,
-        scratch_shapes=[half] * 6 + [
+        scratch_shapes=[
+            pltpu.VMEM((8, 256), jnp.int32),
+            pltpu.VMEM((8, 256), jnp.int32),
+            pltpu.SMEM((8, 256), jnp.int32),
+            pltpu.VMEM((8, 128), jnp.int32),
+        ] + [half] * 6 + [
             pltpu.VMEM((3, RING, CAP, HALF, F), bf),
             pltpu.VMEM((3, RING, CAP, HALF, F), bf),
             pltpu.VMEM((2, RING, 2, HALF, F), bf),
@@ -332,12 +375,11 @@
             pltpu.SemaphoreType.DMA((NCOPY,)),
             pltpu.SemaphoreType.DMA((NRS,)),
             pltpu.SemaphoreType.DMA((NRS,)),
-            pltpu.SemaphoreType.DMA((2,)),
+            pltpu.SemaphoreType.DMA((3,)),
         ],
         compiler_params=pltpu.CompilerParams(
             collective_id=0, has_side_effects=True, vmem_limit_bytes=67043328),
-    )(order, tsel, keep, last, need, need_v,
-      grad_out.reshape(OWN, 2, HALF, F), rel_weight, adjacency)
+    )(type_count, block_row.reshape(1, SLOTS), block_col.reshape(1, SLOTS), grad_out.reshape(OWN, 2, HALF, F), rel_weight, adjacency)
     return out.reshape(OWN * BLK, F)
 
 

time: 106 us -> 77.7 us (0.73)
  Pallas kernels: 91.1 us -> 75.2 us
  other arithmetic: 7.76 us -> 0 us
  between operations: 2.62 us -> 0.01 us
  local copies, waits for them, and re-layouts: 4.33 us -> 2.26 us
    pallas_call x1, Pallas kernels: 91.1 us -> 75.2 us  [per_device(): pl.pallas_call(kernel, out_shape=jax.ShapeDtypeStruct((OWN, BLK, F), jnp....]
    reduce_sum x8 -> x0, other arithmetic: 4.58 us -> none  [the longest x1 0.95 us: plan(): jnp.sum(((block_col[None, :] == block_col[:, None]) & live[None, :] & (k[...]
    slice x1 -> x0, local copies, waits for them, and re-layouts: 1.47 us -> none  [plan(): e3 = e2 + type_count[3]]
    sub x2 -> x0, other arithmetic: 1.17 us -> none  [the longest x1 0.59 us: plan(): order = SLOTS - jnp.sum(jnp.where(oh, SLOTS - k[None, :], 0), axis=1)]
    unnamed x3 -> x1, local copies, waits for them, and re-layouts: 2.27 us -> 2.26 us
where the time goes in v2:
time: 77.7 us; the launch traced here: 77.5 us
  Pallas kernels  75.2 us (97%)
  local copies, waits for them, and re-layouts  2.26 us (3%)
    pallas_call x1, Pallas kernels, per_device(): pl.pallas_call(kernel, out_shape=jax.ShapeDtypeStruct((OWN, BLK, F), jnp....  75.2 us
    unnamed x1, local copies, waits for them, and re-layouts  2.26 us

profile of v2, /device:TPU:1, one launch (start us, length us, event | category | flops | bytes accessed | tf_op | source)
XLA Modules:
  0.0 77.5 jit_solution(7632635567661071318)
XLA Ops:
  0.0 75.2 %shard_map.64 = f32[8,128,256]{2,1,0:T(8,128)} custom-call(s32[4]{0:T(128)} %counts_s.1, s32[1,192]{1,0:T(1,128)} %bitcast.6, s32[1,192]{1,0:T(1,128)} %bitcast.7, bf16[8,2,64,256]{3,2,1,0:T(8,128)(2,1)} %bitcast.5, bf16[4,256,256]{2,1,0:T(8,128)(2,1)} %w_ref.1, bf16[192,128,128]{2,1,0:T(8,128)(2,1)} %a_hbm.1), custom_call_target="tpu_custom_call" | custom-call | tf_op jit(solution)/shard_map/pallas_call | solution.py:344
  75.2 2.3 %copy.8 = f32[1024,256]{1,0:T(8,128)} copy(f32[1024,256]{1,0:T(8,128)} %bitcast.4) | data formatting | bytes 2097152

commit v3 on v2

--- a/solution.py
+++ b/solution.py
@@ -122,6 +122,11 @@
     def got(name):
         copies[name].wait_recv()
 
+    barrier = pltpu.get_barrier_semaphore()
+    greeted = [dev_uv(h, 0, d) for h in (0, 1) for d in (1, 2, 3)] + [dev_z(1), dev_z(3), partner]
+    for dev in greeted:
+        pl.semaphore_signal(barrier, inc=1, device_id=dev, device_id_type=MESH)
+
     a_copy = pltpu.make_async_copy(a_hbm, a_v.at[pl.ds(0, SLOTS)], local_sem.at[0])
     a_copy.start()
 
@@ -134,10 +139,6 @@
     place, need = plan_needs(rows_row)
     need_v[0:1, :] = need
 
-    barrier = pltpu.get_barrier_semaphore()
-    greeted = [dev_uv(h, 0, d) for h in (0, 1) for d in (1, 2, 3)] + [dev_z(1), dev_z(3), partner]
-    for dev in greeted:
-        pl.semaphore_signal(barrier, inc=1, device_id=dev, device_id_type=MESH)
     pl.semaphore_wait(barrier, len(greeted))
 
     for h in (0, 1):
@@ -147,14 +148,6 @@
         for h in (0, 1):
             send(("p1", h, s), g_ref.at[:, h], full[h][4 - s], dev_uv(h, s, 0))
 
-    order, tsel, keep, last = plan_slots(rows_row, cols_row, counts_s, place, y, x)
-    idx_v[0:1, :] = order
-    idx_v[1:2, :] = tsel
-    idx_v[2:3, 0:128] = keep
-    idx_v[3:4, 0:128] = last
-    idx_v[4:5, 0:128] = need
-    idx_copy = pltpu.make_async_copy(idx_v, idx_s, local_sem.at[2])
-    idx_copy.start()
     for t in range(TYPES):
         wt[:, t * F:(t + 1) * F] = w_ref[t].T
     a_v[SLOTS] = jnp.zeros((BLK, BLK), jnp.bfloat16)
@@ -166,7 +159,6 @@
     need_copy = pltpu.make_async_copy(needs_v, needs_s, local_sem.at[1])
     need_copy.start()
     need_copy.wait()
-    idx_copy.wait()
 
     def pick(h, du, b):
         return g_ref[b, h] if du == 0 else full[h][du][b]
@@ -228,8 +220,14 @@
 
     push(0, 0)
     push(1, 0)
-    make_table(0, 0)
-    a_copy.wait()
+    order, tsel, keep, last = plan_slots(rows_row, cols_row, counts_s, place, y, x)
+    idx_v[0:1, :] = order
+    idx_v[1:2, :] = tsel
+    idx_v[2:3, 0:128] = keep
+    idx_v[3:4, 0:128] = last
+    idx_v[4:5, 0:128] = need
+    idx_copy = pltpu.make_async_copy(idx_v, idx_s, local_sem.at[2])
+    idx_copy.start()
     for s in (1, 3):
         for h in (0, 1):
             got(("p1", h, s))
@@ -238,26 +236,33 @@
     for du in (3, 1):
         push(0, du)
         push(1, du)
+    idx_copy.wait()
+    make_table(0, 0)
     forward(0, 0)
     forward(1, 0)
-    turn(0, 48)
+    a_copy.wait()
+    turn(0, 16)
     for h in (0, 1):
         for s in (1, 3):
             got(("p1r", h, s))
-    push(0, 2)
-    push(1, 2)
+        push(h, 2)
     for dy, dx in ((0, 1), (0, 3), (1, 0), (3, 0)):
         make_table(dy, dx)
-    for du in (3, 1):
-        forward(0, du)
-        forward(1, du)
-    turn(48, 96)
+    turn(16, 32)
+    forward(0, 3)
+    forward(1, 3)
+    turn(32, 56)
+    forward(0, 1)
+    forward(1, 1)
+    make_table(0, 2)
+    make_table(2, 0)
+    turn(56, 80)
     for dy, dx in ((1, 1), (1, 3), (3, 1), (3, 3)):
         make_table(dy, dx)
     forward(0, 2)
     forward(1, 2)
-    turn(96, PAIRS)
-    for dy, dx in ((0, 2), (2, 0), (1, 2), (3, 2), (2, 1), (2, 3), (2, 2)):
+    turn(80, PAIRS)
+    for dy, dx in ((1, 2), (3, 2), (2, 1), (2, 3), (2, 2)):
         make_table(dy, dx)
 
     acc[...] = jnp.zeros_like(acc)

time: 77.7 us -> 80.9 us (1.041)
  Pallas kernels: 75.2 us -> 78.4 us
    pallas_call x1, Pallas kernels: 75.2 us -> 78.4 us  [per_device(): pl.pallas_call(kernel, out_shape=jax.ShapeDtypeStruct((OWN, BLK, F), jnp....]
where the time goes in v3:
time: 80.9 us; the launch traced here: 80.7 us
  Pallas kernels  78.4 us (97%)
  local copies, waits for them, and re-layouts  2.26 us (3%)
    pallas_call x1, Pallas kernels, per_device(): pl.pallas_call(kernel, out_shape=jax.ShapeDtypeStruct((OWN, BLK, F), jnp....  78.4 us
    unnamed x1, local copies, waits for them, and re-layouts  2.26 us

profile of v3, /device:TPU:1, one launch (start us, length us, event | category | flops | bytes accessed | tf_op | source)
XLA Modules:
  0.0 80.7 jit_solution(16466382455542537920)
XLA Ops:
  0.0 78.4 %shard_map.64 = f32[8,128,256]{2,1,0:T(8,128)} custom-call(s32[4]{0:T(128)} %counts_s.1, s32[1,192]{1,0:T(1,128)} %bitcast.6, s32[1,192]{1,0:T(1,128)} %bitcast.7, bf16[8,2,64,256]{3,2,1,0:T(8,128)(2,1)} %bitcast.5, bf16[4,256,256]{2,1,0:T(8,128)(2,1)} %w_ref.1, bf16[192,128,128]{2,1,0:T(8,128)(2,1)} %a_hbm.1), custom_call_target="tpu_custom_call" | custom-call | tf_op jit(solution)/shard_map/pallas_call | solution.py:349
  78.4 2.3 %copy.8 = f32[1024,256]{1,0:T(8,128)} copy(f32[1024,256]{1,0:T(8,128)} %bitcast.4) | data formatting | bytes 2097152

commit v4 on v2

--- a/solution.py
+++ b/solution.py
@@ -17,7 +17,7 @@
 PAIRS = 128
 COLS = 64
 NCOPY = 62
-NRS = 10
+NRS = 13
 
 
 def across(row_vec, depth):
@@ -79,8 +79,8 @@
     return order, tsel, 1 - first, last
 
 
-def kernel(counts_s, rows_ref, cols_ref, g_ref, w_ref, a_hbm, out_ref,
-           rc_v, idx_v, idx_s, need_v,
+def kernel(counts_s, rows_ref, cols_ref, g_hbm, w_hbm, a_hbm, out_hbm,
+           g_ref, w_ref, out_ref, rc_v, idx_v, idx_s, need_v,
            g01, g02, g03, g11, g12, g13, p0, p1, rl0, rl1, pk0, pk1, needs_v, needs_s,
            wt, a_v, at, table, acc, prefix, ps, pr, ss, zr, zf,
            send_sem, recv_sem, rs_send, rs_recv, local_sem):
@@ -122,6 +122,15 @@
     def got(name):
         copies[name].wait_recv()
 
+    barrier = pltpu.get_barrier_semaphore()
+    greeted = [dev_uv(h, 0, d) for h in (0, 1) for d in (1, 2, 3)] + [dev_z(1), dev_z(3), partner]
+    for dev in greeted:
+        pl.semaphore_signal(barrier, inc=1, device_id=dev, device_id_type=MESH)
+
+    g_copy = pltpu.make_async_copy(g_hbm, g_ref, local_sem.at[3])
+    g_copy.start()
+    w_copy = pltpu.make_async_copy(w_hbm, w_ref, local_sem.at[4])
+    w_copy.start()
     a_copy = pltpu.make_async_copy(a_hbm, a_v.at[pl.ds(0, SLOTS)], local_sem.at[0])
     a_copy.start()
 
@@ -134,10 +143,7 @@
     place, need = plan_needs(rows_row)
     need_v[0:1, :] = need
 
-    barrier = pltpu.get_barrier_semaphore()
-    greeted = [dev_uv(h, 0, d) for h in (0, 1) for d in (1, 2, 3)] + [dev_z(1), dev_z(3), partner]
-    for dev in greeted:
-        pl.semaphore_signal(barrier, inc=1, device_id=dev, device_id_type=MESH)
+    g_copy.wait()
     pl.semaphore_wait(barrier, len(greeted))
 
     for h in (0, 1):
@@ -155,6 +161,7 @@
     idx_v[4:5, 0:128] = need
     idx_copy = pltpu.make_async_copy(idx_v, idx_s, local_sem.at[2])
     idx_copy.start()
+    w_copy.wait()
     for t in range(TYPES):
         wt[:, t * F:(t + 1) * F] = w_ref[t].T
     a_v[SLOTS] = jnp.zeros((BLK, BLK), jnp.bfloat16)
@@ -289,33 +296,35 @@
         rs[name] = c
 
     f32 = jnp.float32
-    for dz in (2, 1, 3, 0):
-        for b in range(OWN):
+    for dz, lo, n in ((2, 0, 4), (2, 4, 4), (1, 4, 4), (3, 0, 4), (1, 0, 4), (3, 4, 4), (0, 0, 8)):
+        for b in range(lo, lo + n):
             ps[dz, b] = mine(dz, 1 - core, b)
-        rsend(("pair", dz), ps.at[dz], pr.at[dz], partner)
-
-    rs[("pair", 2)].wait_recv()
-    for b in range(OWN):
-        ss[1, b] = (mine(2, core, b).astype(f32) + pr[2, b].astype(f32)).astype(jnp.bfloat16)
+        rsend(("pair", dz, lo), ps.at[dz, pl.ds(lo, n)], pr.at[dz, pl.ds(lo, n)], partner)
+
+    def both(dz, lo):
+        rs[("pair", dz, lo)].wait_recv()
+        for b in range(lo, lo + 4):
+            ss[dz - 1, b] = (mine(dz, core, b).astype(f32) + pr[dz, b].astype(f32)).astype(jnp.bfloat16)
+
+    both(2, 0)
     rsend("far0", ss.at[1, pl.ds(0, 4)], zr.at[0], dev_z(1))
+    both(2, 4)
     rsend("far1", ss.at[1, pl.ds(4, 4)], zr.at[1], dev_z(3))
-    rs[("pair", 1)].wait_recv()
-    for b in range(4, 8):
-        ss[0, b] = (mine(1, core, b).astype(f32) + pr[1, b].astype(f32)).astype(jnp.bfloat16)
+    both(1, 4)
     rsend("up_b", ss.at[0, pl.ds(4, 4)], zf.at[0, pl.ds(4, 4)], dev_z(1))
-    rs[("pair", 3)].wait_recv()
-    for b in range(0, 4):
-        ss[2, b] = (mine(3, core, b).astype(f32) + pr[3, b].astype(f32)).astype(jnp.bfloat16)
+    both(3, 0)
     rsend("down_a", ss.at[2, pl.ds(0, 4)], zf.at[1, pl.ds(0, 4)], dev_z(3))
+    rs[("pair", 1, 0)].wait_recv()
     rs["far0"].wait_recv()
     for b in range(0, 4):
         ss[0, b] = (mine(1, core, b).astype(f32) + pr[1, b].astype(f32) + zr[0, b].astype(f32)).astype(jnp.bfloat16)
     rsend("up_a", ss.at[0, pl.ds(0, 4)], zf.at[0, pl.ds(0, 4)], dev_z(1))
+    rs[("pair", 3, 4)].wait_recv()
     rs["far1"].wait_recv()
     for b in range(4, 8):
         ss[2, b] = (mine(3, core, b).astype(f32) + pr[3, b].astype(f32) + zr[1, b - 4].astype(f32)).astype(jnp.bfloat16)
     rsend("down_b", ss.at[2, pl.ds(4, 4)], zf.at[1, pl.ds(4, 4)], dev_z(3))
-    rs[("pair", 0)].wait_recv()
+    rs[("pair", 0, 0)].wait_recv()
     for b in range(OWN):
         out_ref[b] = mine(0, core, b).astype(f32) + pr[0, b].astype(f32)
     rs["up_b"].wait_recv()
@@ -327,26 +336,35 @@
     rs["up_a"].wait_recv()
     for b in range(0, 4):
         out_ref[b] = out_ref[b] + zf[0, b].astype(f32)
+    outs = [pltpu.make_async_copy(out_ref.at[pl.ds(lo, 4)], out_hbm.at[pl.ds(lo, 4)], local_sem.at[5 + lo // 4]) for lo in (0, 4)]
+    outs[0].start()
     rs["down_b"].wait_recv()
     for b in range(4, 8):
         out_ref[b] = out_ref[b] + zf[1, b].astype(f32)
+    outs[1].start()
     for c in copies.values():
         c.wait_send()
     for c in rs.values():
         c.wait_send()
+    for c in outs:
+        c.wait()
 
 
 def per_device(grad_out, rel_weight, adjacency, block_row, block_col, type_count):
     bf = jnp.bfloat16
     smem = pl.BlockSpec(memory_space=pltpu.SMEM)
     vmem = pl.BlockSpec(memory_space=pltpu.VMEM)
+    hbm = pl.BlockSpec(memory_space=pltpu.HBM)
     half = pltpu.VMEM((OWN, HALF, F), bf)
     out = pl.pallas_call(
         kernel,
         out_shape=jax.ShapeDtypeStruct((OWN, BLK, F), jnp.float32),
-        in_specs=[smem] + [vmem] * 4 + [pl.BlockSpec(memory_space=pl.ANY)],
-        out_specs=vmem,
+        in_specs=[smem] + [vmem] * 2 + [hbm] * 3,
+        out_specs=hbm,
         scratch_shapes=[
+            pltpu.VMEM((OWN, 2, HALF, F), bf),
+            pltpu.VMEM((TYPES, F, F), bf),
+            pltpu.VMEM((OWN, BLK, F), jnp.float32),
             pltpu.VMEM((8, 256), jnp.int32),
             pltpu.VMEM((8, 256), jnp.int32),
             pltpu.SMEM((8, 256), jnp.int32),
@@ -375,7 +393,7 @@
             pltpu.SemaphoreType.DMA((NCOPY,)),
             pltpu.SemaphoreType.DMA((NRS,)),
             pltpu.SemaphoreType.DMA((NRS,)),
-            pltpu.SemaphoreType.DMA((3,)),
+            pltpu.SemaphoreType.DMA((7,)),
         ],
         compiler_params=pltpu.CompilerParams(
             collective_id=0, has_side_effects=True, vmem_limit_bytes=67043328),

time: 77.7 us -> 76.7 us (0.987)
  Pallas kernels: 75.2 us -> 74.3 us
    pallas_call x1, Pallas kernels: 75.2 us -> 74.3 us  [per_device(): pl.pallas_call(kernel, out_shape=jax.ShapeDtypeStruct((OWN, BLK, F), jnp....]
where the time goes in v4:
time: 76.7 us; the launch traced here: 76.5 us
  Pallas kernels  74.3 us (97%)
  local copies, waits for them, and re-layouts  2.26 us (3%)
    pallas_call x1, Pallas kernels, per_device(): pl.pallas_call(kernel, out_shape=jax.ShapeDtypeStruct((OWN, BLK, F), jnp....  74.3 us
    unnamed x1, local copies, waits for them, and re-layouts  2.26 us

profile of v4, /device:TPU:1, one launch (start us, length us, event | category | flops | bytes accessed | tf_op | source)
XLA Modules:
  0.0 76.5 jit_solution(16327235644212711362)
XLA Ops:
  0.0 74.3 %shard_map.64 = f32[8,128,256]{2,1,0:T(8,128)} custom-call(s32[4]{0:T(128)} %counts_s.1, s32[1,192]{1,0:T(1,128)} %bitcast.6, s32[1,192]{1,0:T(1,128)} %bitcast.7, bf16[8,2,64,256]{3,2,1,0:T(8,128)(2,1)} %bitcast.5, bf16[4,256,256]{2,1,0:T(8,128)(2,1)} %w_hbm.1, bf16[192,128,128]{2,1,0:T(8,128)(2,1)} %a_hbm.1), custom_call_target="tpu_custom_call" | custom-call | tf_op jit(solution)/shard_map/pallas_call | solution.py:359
  74.3 2.3 %copy.8 = f32[1024,256]{1,0:T(8,128)} copy(f32[1024,256]{1,0:T(8,128)} %bitcast.4) | data formatting | bytes 2097152

commit v5 on v4

--- a/solution.py
+++ b/solution.py
@@ -333,15 +333,12 @@
     rs["down_a"].wait_recv()
     for b in range(0, 4):
         out_ref[b] = out_ref[b] + zf[1, b].astype(f32)
-    rs["up_a"].wait_recv()
-    for b in range(0, 4):
-        out_ref[b] = out_ref[b] + zf[0, b].astype(f32)
-    outs = [pltpu.make_async_copy(out_ref.at[pl.ds(lo, 4)], out_hbm.at[pl.ds(lo, 4)], local_sem.at[5 + lo // 4]) for lo in (0, 4)]
-    outs[0].start()
-    rs["down_b"].wait_recv()
-    for b in range(4, 8):
-        out_ref[b] = out_ref[b] + zf[1, b].astype(f32)
-    outs[1].start()
+    outs = [pltpu.make_async_copy(out_ref.at[b], out_hbm.at[pl.ds(b * BLK, BLK)], local_sem.at[5 + b]) for b in range(OWN)]
+    for name, zi, lo in (("up_a", 0, 0), ("down_b", 1, 4)):
+        rs[name].wait_recv()
+        for b in range(lo, lo + 4):
+            out_ref[b] = out_ref[b] + zf[zi, b].astype(f32)
+            outs[b].start()
     for c in copies.values():
         c.wait_send()
     for c in rs.values():
@@ -356,9 +353,9 @@
     vmem = pl.BlockSpec(memory_space=pltpu.VMEM)
     hbm = pl.BlockSpec(memory_space=pltpu.HBM)
     half = pltpu.VMEM((OWN, HALF, F), bf)
-    out = pl.pallas_call(
+    return pl.pallas_call(
         kernel,
-        out_shape=jax.ShapeDtypeStruct((OWN, BLK, F), jnp.float32),
+        out_shape=jax.ShapeDtypeStruct((OWN * BLK, F), jnp.float32),
         in_specs=[smem] + [vmem] * 2 + [hbm] * 3,
         out_specs=hbm,
         scratch_shapes=[
@@ -393,12 +390,11 @@
             pltpu.SemaphoreType.DMA((NCOPY,)),
             pltpu.SemaphoreType.DMA((NRS,)),
             pltpu.SemaphoreType.DMA((NRS,)),
-            pltpu.SemaphoreType.DMA((7,)),
+            pltpu.SemaphoreType.DMA((5 + OWN,)),
         ],
         compiler_params=pltpu.CompilerParams(
             collective_id=0, has_side_effects=True, vmem_limit_bytes=67043328),
     )(type_count, block_row.reshape(1, SLOTS), block_col.reshape(1, SLOTS), grad_out.reshape(OWN, 2, HALF, F), rel_weight, adjacency)
-    return out.reshape(OWN * BLK, F)
 
 
 def solution(mesh):

time: 76.7 us -> 76.7 us (level)
  no operation moved by 1% of the time
where the time goes in v5:
time: 76.7 us; the launch traced here: 76.6 us
  Pallas kernels  74.3 us (97%)
  local copies, waits for them, and re-layouts  2.26 us (3%)
    pallas_call x1, Pallas kernels, per_device(): pl.pallas_call(kernel, out_shape=jax.ShapeDtypeStruct((OWN * BLK, F), jnp...  74.3 us
    unnamed x1, local copies, waits for them, and re-layouts  2.26 us

profile of v5, /device:TPU:1, one launch (start us, length us, event | category | flops | bytes accessed | tf_op | source)
XLA Modules:
  0.0 76.6 jit_solution(676871397232804904)
XLA Ops:
  0.0 74.3 %shard_map.64 = f32[1024,256]{1,0:T(8,128)} custom-call(s32[4]{0:T(128)} %counts_s.1, s32[1,192]{1,0:T(1,128)} %bitcast.4, s32[1,192]{1,0:T(1,128)} %bitcast.5, bf16[8,2,64,256]{3,2,1,0:T(8,128)(2,1)} %bitcast.3, bf16[4,256,256]{2,1,0:T(8,128)(2,1)} %w_hbm.1, bf16[192,128,128]{2,1,0:T(8,128)(2,1)} %a_hbm.1), custom_call_target="tpu_custom_call" | custom-call | tf_op jit(solution)/shard_map/pallas_call | solution.py:356
  74.3 2.3 %copy.8 = f32[1024,256]{1,0:T(8,128)} copy(f32[1024,256]{1,0:T(8,128)} %shard_map.64) | data formatting | bytes 2097152

commit v6 on v5

--- a/solution.py
+++ b/solution.py
@@ -80,7 +80,7 @@
 
 
 def kernel(counts_s, rows_ref, cols_ref, g_hbm, w_hbm, a_hbm, out_hbm,
-           g_ref, w_ref, out_ref, rc_v, idx_v, idx_s, need_v,
+           g_ref, w_ref, out_ref, out_b, rc_v, idx_v, idx_s, need_v,
            g01, g02, g03, g11, g12, g13, p0, p1, rl0, rl1, pk0, pk1, needs_v, needs_s,
            wt, a_v, at, table, acc, prefix, ps, pr, ss, zr, zf,
            send_sem, recv_sem, rs_send, rs_recv, local_sem):
@@ -333,11 +333,11 @@
     rs["down_a"].wait_recv()
     for b in range(0, 4):
         out_ref[b] = out_ref[b] + zf[1, b].astype(f32)
-    outs = [pltpu.make_async_copy(out_ref.at[b], out_hbm.at[pl.ds(b * BLK, BLK)], local_sem.at[5 + b]) for b in range(OWN)]
+    outs = [pltpu.make_async_copy(out_b.at[b], out_hbm.at[pl.ds(b * BLK, BLK)], local_sem.at[5 + b]) for b in range(OWN)]
     for name, zi, lo in (("up_a", 0, 0), ("down_b", 1, 4)):
         rs[name].wait_recv()
         for b in range(lo, lo + 4):
-            out_ref[b] = out_ref[b] + zf[zi, b].astype(f32)
+            out_b[b] = (out_ref[b] + zf[zi, b].astype(f32)).astype(jnp.bfloat16)
             outs[b].start()
     for c in copies.values():
         c.wait_send()
@@ -353,15 +353,16 @@
     vmem = pl.BlockSpec(memory_space=pltpu.VMEM)
     hbm = pl.BlockSpec(memory_space=pltpu.HBM)
     half = pltpu.VMEM((OWN, HALF, F), bf)
-    return pl.pallas_call(
+    out = pl.pallas_call(
         kernel,
-        out_shape=jax.ShapeDtypeStruct((OWN * BLK, F), jnp.float32),
+        out_shape=jax.ShapeDtypeStruct((OWN * BLK, F), bf),
         in_specs=[smem] + [vmem] * 2 + [hbm] * 3,
         out_specs=hbm,
         scratch_shapes=[
             pltpu.VMEM((OWN, 2, HALF, F), bf),
             pltpu.VMEM((TYPES, F, F), bf),
             pltpu.VMEM((OWN, BLK, F), jnp.float32),
+            pltpu.VMEM((OWN, BLK, F), bf),
             pltpu.VMEM((8, 256), jnp.int32),
             pltpu.VMEM((8, 256), jnp.int32),
             pltpu.SMEM((8, 256), jnp.int32),
@@ -395,6 +396,7 @@
         compiler_params=pltpu.CompilerParams(
             collective_id=0, has_side_effects=True, vmem_limit_bytes=67043328),
     )(type_count, block_row.reshape(1, SLOTS), block_col.reshape(1, SLOTS), grad_out.reshape(OWN, 2, HALF, F), rel_weight, adjacency)
+    return out.astype(jnp.float32)
 
 
 def solution(mesh):

time: 76.7 us -> 76.3 us (level)
  local copies, waits for them, and re-layouts: 2.26 us -> 0 us
  other arithmetic: 0 us -> 2.09 us
    unnamed x1 -> x0, local copies, waits for them, and re-layouts: 2.26 us -> none
    convert_element_type x0 -> x1, other arithmetic: none -> 2.09 us  [per_device(): return out.astype(jnp.float32)]
where the time goes in v6:
time: 76.3 us; the launch traced here: 76.2 us
  Pallas kernels  74.1 us (97%)
  other arithmetic  2.09 us (3%)
    pallas_call x1, Pallas kernels, per_device(): pl.pallas_call(kernel, out_shape=jax.ShapeDtypeStruct((OWN * BLK, F), bf)...  74.1 us
    convert_element_type x1, other arithmetic, per_device(): return out.astype(jnp.float32)  2.09 us

profile of v6, /device:TPU:1, one launch (start us, length us, event | category | flops | bytes accessed | tf_op | source)
XLA Modules:
  0.0 76.2 jit_solution(11205518235061137900)
XLA Ops:
  0.0 74.1 %shard_map.64 = bf16[1024,256]{1,0:T(8,128)(2,1)} custom-call(s32[4]{0:T(128)} %counts_s.1, s32[1,192]{1,0:T(1,128)} %bitcast.4, s32[1,192]{1,0:T(1,128)} %bitcast.5, bf16[8,2,64,256]{3,2,1,0:T(8,128)(2,1)} %bitcast.3, bf16[4,256,256]{2,1,0:T(8,128)(2,1)} %w_hbm.1, bf16[192,128,128]{2,1,0:T(8,128)(2,1)} %a_hbm.1), custom_call_target="tpu_custom_call" | custom-call | tf_op jit(solution)/shard_map/pallas_call | solution.py:356
  74.1 2.1 %convert_element_type.3 = f32[1024,256]{1,0:T(8,128)} convert(bf16[1024,256]{1,0:T(8,128)(2,1)} %shard_map.64) | non-fusion elementwise | flops 262144 | bytes 1572864 | tf_op jit(solution)/shard_map/convert_element_type | solution.py:399
